TPU v7x, 64 devices: a 2x2x8 block of a 4x4x8 slice. The times are simulated.
64 devices in a mesh: rep: 4 (over x, y), dp: 16 (over z, core).
Axes of the slice: x: 2, y: 2, z: 8, core: 2. Of those that a mesh axis runs over, the one named last changes fastest.
The devices are a block of a 4x4x8 slice.
Arguments:
- a: bfloat16 [64, 4, 4096, 640], P(('rep', 'dp')), parts along dimension 0
- g: bfloat16 [64, 4, 4096, 2560], P(('rep', 'dp')), parts along dimension 0
Outputs:
- output: bfloat16 [16, 640, 2560], P('rep'), parts along dimension 0
There are 4 independent parts. A program takes and returns all parts, laid end to end along the dimension named above; each array names one.
All inputs are finite; a program needn't handle non-finite values.
Results may differ from a plain program's by a relative error of at most 0.012.
Values are sent between devices in bfloat16 or wider.
A program may use at most 768 MiB of HBM per device.

v0:
```python
import jax
import jax.numpy as jnp


def solution(mesh):
    groups = mesh.shape["rep"]

    def step(a, g):
        a, g = (t.reshape(groups, -1, *t.shape[1:]) for t in (a, g))
        sums = jnp.einsum("rsntd,rsntf->rndf", a, g, preferred_element_type=jnp.float32)
        return sums.astype(jnp.bfloat16).reshape(-1, *sums.shape[2:])

    return step
```

profile of v0, /device:TPU:21, one launch (start us, length us, event | category | flops | bytes accessed | tf_op | source)
XLA Modules:
  0.0 357.7 jit_solution(17035291150952588060)
XLA Ops:
  0.0 64.2 %fusion.3 = f32[1,4,640,2560]{3,2,1,0:T(8,128)} fusion(bf16[1,4,4096,2560]{3,2,1,0:T(8,128)(2,1)} %param.1, bf16[1,4,4096,640]{3,2,1,0:T(8,128)(2,1)} %param), kind=kOutput, calls=%fused_computation.4 | convolution fusion | flops 53687091200 | bytes 131072000 | tf_op jit(solution)/rsntd,rsntf->rndf/dot_general | solution.py:10
  64.2 293.5 %all-reduce.2 = bf16[1,4,640,2560]{3,2,1,0:T(8,128)(2,1)} all-reduce(f32[1,4,640,2560]{3,2,1,0:T(8,128)} %fusion.3), channel_id=1, replica_groups=[4,16]<=[64], use_global_device_ids=true, to_apply=%add.clone | all-reduce | flops 6553600 | bytes 39321600 | tf_op jit(solution)/rsntd,rsntf->rndf/dot_general | solution.py:10
where the time goes:
time: 358 us
  blocking collectives  293 us (82%)
  matrix products  64.2 us (18%)
    dot_general x1, blocking collectives, step(): jnp.einsum('rsntd,rsntf->rndf', a, g, preferred_element_type=jnp.float32)  293 us
    dot_general x1, matrix products, step(): jnp.einsum('rsntd,rsntf->rndf', a, g, preferred_element_type=jnp.float32)  64.2 us

commit v1 on v0

v1 whole, which is shorter than its diff:
```python
import functools

import jax
import jax.numpy as jnp
from jax import lax
from jax.experimental import pallas as pl
from jax.experimental.pallas import tpu as pltpu
from jax.sharding import PartitionSpec as P

MESH = pl.DeviceIdType.MESH
F32 = jnp.float32
BF16 = jnp.bfloat16


def sizes(n, a_shape, g_shape):
    mats, tokens, d = a_shape
    ff = g_shape[2]
    chips = n // 2
    assert chips == 2 * mats and mats == 4
    width = ff * mats // chips
    tile = 256 if width % 256 == 0 else 128
    return dict(
        mats=mats, tokens=tokens, d=d, ff=ff, chips=chips, half=d // 2, width=width, tile=tile,
        tiles=width // tile, chunk=tokens // 8, chunks=8,
    )


def sum_kernel(n, s, a_hbm, g_hbm, out, at, araw, gbuf, part, part_half, land, head, psend, acc,
               a_sem, g_sem, ps_sem, pr_sem, rs_send, rs_recv, ag_send, ag_recv, ad_send, ad_recv):
    mats, chips, half, tile, tiles = s["mats"], s["chips"], s["half"], s["tile"], s["tiles"]
    d, width, chunk, chunks = s["d"], s["width"], s["chunk"], s["chunks"]
    far = chips // 2
    depth = gbuf.shape[0]
    me = lax.axis_index("dp")
    core = me % 2
    c = me // 2
    sgn = 2 * core - 1
    nxt = {"dp": ((c + sgn + chips) % chips) * 2 + core}
    prv = {"dp": ((c - sgn + chips) % chips) * 2 + core}
    partner = {"dp": c * 2 + 1 - core}
    mine = pl.multiple_of(core * half, half)
    other = pl.multiple_of((1 - core) * half, half)
    big = 8 * chips

    def shard(r):
        return (c + sgn * r + big) % chips

    def slot_of(r):
        return (r + big) % mats

    def columns(j, i):
        return pl.ds(pl.multiple_of((j // mats) * width + i * tile, tile), tile)

    def a_copy(slot, r):
        m = (c + sgn * slot + big) % mats
        return pltpu.make_async_copy(
            a_hbm.at[m, pl.ds(pl.multiple_of(r * chunk, chunk), chunk)], araw.at[r], a_sem.at[r])

    def g_copy(q, j, i):
        b = q % depth
        return pltpu.make_async_copy(g_hbm.at[j % mats, :, columns(j, i)], gbuf.at[b], g_sem.at[b])

    def g_start(q):
        @pl.when(q < tiles)
        def _():
            g_copy(q, shard(far), q).start()

        @pl.when((q >= tiles) & (q < tiles * 7))
        def _():
            r = q - tiles
            k = 3 - r // (2 * tiles)
            w = r % (2 * tiles)
            g_copy(q, shard(k * (2 * (w % 2) - 1)), w // 2).start()

        @pl.when((q >= tiles * 7) & (q < tiles * 8))
        def _():
            g_copy(q, shard(0), q - tiles * 7).start()

    def g_wait(q):
        g_copy(q, 0, 0).wait()

    def transpose(slot, r):
        a_copy(slot, r).wait()
        at[slot, :, pl.ds(pl.multiple_of(r * chunk, chunk), chunk)] = araw[r].T

    def dot(slot, row, rows, q):
        return jnp.dot(at[slot, pl.ds(row, rows), :], gbuf[q % depth], preferred_element_type=F32)

    def to_partner(src, dst, u, k, i):
        return pltpu.make_async_remote_copy(
            src, dst, ps_sem.at[u], pr_sem.at[k, i], device_id=partner, device_id_type=MESH)

    def full_p(u, k, i):
        return to_partner(psend.at[u], part.at[k - 1, i], u, k, i)

    def half_p(u, k, i):
        return to_partner(psend.at[u, pl.ds(0, half)], part_half.at[k // far, i], u, k, i)

    def rs_head(i):
        return pltpu.make_async_remote_copy(
            head.at[i], land.at[far - 1, i, pl.ds(mine, half)], rs_send.at[far - 1, i],
            rs_recv.at[far - 1, i], device_id=nxt, device_id_type=MESH)

    def rs_full(k, i):
        return pltpu.make_async_remote_copy(
            land.at[k, i], land.at[k - 1, i], rs_send.at[k - 1, i], rs_recv.at[k - 1, i],
            device_id=nxt, device_id_type=MESH)

    def block(ref, j, row, i):
        return ref.at[j % mats, pl.ds(row, half), columns(j, i)]

    def ag(h, i):
        b = block(out, shard(-(h - 1)), mine, i)
        return pltpu.make_async_remote_copy(
            b, b, ag_send.at[h - 1, i], ag_recv.at[h - 1, i], device_id=nxt, device_id_type=MESH)

    def ag_arrival(h, i):
        b = block(out, shard(-h), mine, i)
        return pltpu.make_async_remote_copy(
            b, b, ag_send.at[h - 1, i], ag_recv.at[h - 1, i], device_id=nxt, device_id_type=MESH)

    def across(h, i):
        b = block(out, shard(-h), mine, i)
        return pltpu.make_async_remote_copy(
            b, b, ad_send.at[h, i], ad_recv.at[h, i], device_id=partner, device_id_type=MESH)

    def across_arrival(h, i):
        b = block(out, shard(h), other, i)
        return pltpu.make_async_remote_copy(
            b, b, ad_send.at[h, i], ad_recv.at[h, i], device_id=partner, device_id_type=MESH)

    for r in range(chunks):
        a_copy(0, r).start()
    g_start(0)
    g_start(1)
    barrier = pltpu.get_barrier_semaphore()
    for peer in (nxt, prv, partner):
        pl.semaphore_signal(barrier, 1, device_id=peer, device_id_type=MESH)
    pl.semaphore_wait(barrier, 3)

    def first(r, _):
        transpose(0, r)
        a_copy(1, r).start()
        return 0

    lax.fori_loop(0, chunks, first, 0)

    def head_out(i):
        half_p(i % 2, far, i).wait_recv()
        head[i] = (acc[pl.ds(0, half)] + part_half[1, i].astype(F32)).astype(BF16)
        rs_head(i).start()

    def phase_far(i, _):
        g_start(i + 2)
        g_wait(i)

        @pl.when(i >= 2)
        def _():
            half_p(i % 2, far, i).wait_send()

        psend[i % 2, pl.ds(0, half)] = dot(0, other, half, i).astype(BF16)
        half_p(i % 2, far, i).start()

        @pl.when(i >= 1)
        def _():
            head_out(i - 1)

        acc[pl.ds(0, half)] = dot(0, mine, half, i)

        @pl.when(i < 4)
        def _():
            for u in range(4):
                r = (4 * i + u) % chunks
                transpose(1 + 2 * (i // 2), r)
                a_copy(3 - i // 2, r).start()
        return 0

    lax.fori_loop(0, tiles, phase_far, 0)
    head_out(tiles - 1)
    for u in range(2):
        half_p(u, far, 0).wait_send()

    def phase(t, _):
        k = 3 - t // tiles
        i = t % tiles
        q = tiles + 2 * t
        g_start(q + 2)
        g_wait(q)

        @pl.when(t >= 2)
        def _():
            full_p(t % 2, k, i).wait_send()

        psend[t % 2] = dot(slot_of(-k), 0, d, q).astype(BF16)
        full_p(t % 2, k, i).start()

        @pl.when(t < 4)
        def _():
            for u in range(2):
                transpose(2, 2 * t + u)

        g_start(q + 3)
        g_wait(q + 1)
        acc[...] = dot(slot_of(k), 0, d, q + 1)
        full_p(t % 2, k, i).wait_recv()

        @pl.when(k == 3)
        def _():
            rs_head(i).wait_recv()
            land[k, i, pl.ds(mine, half)] = (
                acc[pl.ds(mine, half)] + part[k - 1, i, pl.ds(mine, half)].astype(F32)
                + land[k, i, pl.ds(mine, half)].astype(F32)).astype(BF16)
            land[k, i, pl.ds(other, half)] = (
                acc[pl.ds(other, half)] + part[k - 1, i, pl.ds(other, half)].astype(F32)).astype(BF16)

        @pl.when(k < 3)
        def _():
            rs_full(k + 1, i).wait_recv()
            land[k, i] = (acc[...] + part[k - 1, i].astype(F32) + land[k, i].astype(F32)).astype(BF16)

        rs_full(k, i).start()
        return 0

    lax.fori_loop(0, 3 * tiles, phase, 0)
    for u in range(2):
        full_p(u, 1, 0).wait_send()

    def own_out(i):
        half_p(i % 2, 0, i).wait_recv()
        j = shard(0)
        out[j % mats, pl.ds(mine, half), columns(j, i)] = (
            acc[pl.ds(0, half)] + part_half[0, i].astype(F32)).astype(BF16)
        ag(1, i).start()
        across(0, i).start()

    def phase_own(i, _):
        q = 7 * tiles + i
        g_start(q + 2)
        g_wait(q)

        @pl.when(i >= 2)
        def _():
            half_p(i % 2, 0, i).wait_send()

        rs_full(1, i).wait_recv()
        psend[i % 2, pl.ds(0, half)] = (
            dot(0, other, half, q) + land[0, i, pl.ds(other, half)].astype(F32)).astype(BF16)
        half_p(i % 2, 0, i).start()

        @pl.when(i >= 1)
        def _():
            own_out(i - 1)

        acc[pl.ds(0, half)] = dot(0, mine, half, q) + land[0, i, pl.ds(mine, half)].astype(F32)
        return 0

    lax.fori_loop(0, tiles, phase_own, 0)
    own_out(tiles - 1)
    for u in range(2):
        half_p(u, 0, 0).wait_send()

    def gather(t, _):
        h = 1 + t // tiles
        i = t % tiles
        ag_arrival(h, i).wait_recv()

        @pl.when(h < chips - 1)
        def _():
            ag(h + 1, i).start()

        across(h, i).start()
        return 0

    lax.fori_loop(0, (chips - 1) * tiles, gather, 0)

    def drain(t, _):
        k = t // tiles
        i = t % tiles
        across_arrival(k, i).wait_recv()
        across(k, i).wait_send()

        @pl.when(k < chips - 1)
        def _():
            ag(k + 1, i).wait_send()

        @pl.when(k < 3)
        def _():
            rs_full(k + 1, i).wait_send()

        @pl.when(k == 3)
        def _():
            rs_head(i).wait_send()
        return 0

    lax.fori_loop(0, chips * tiles, drain, 0)


def store_kernel(x, o, sem):
    parts = [pltpu.make_async_copy(x.at[m], o.at[m], sem.at[m]) for m in range(x.shape[0])]
    for p in parts:
        p.start()
    for p in parts:
        p.wait()


def solution(mesh):
    n = mesh.shape["dp"]
    any_spec = pl.BlockSpec(memory_space=pl.ANY)
    vmem_spec = pl.BlockSpec(memory_space=pltpu.VMEM)

    def step(a, g):
        a, g = a[0], g[0]
        s = sizes(n, a.shape, g.shape)
        d, half, tile, tiles, chips = s["d"], s["half"], s["tile"], s["tiles"], s["chips"]
        shape = (s["mats"], d, s["ff"])
        dma = pltpu.SemaphoreType.DMA
        sums = pl.pallas_call(
            functools.partial(sum_kernel, n, s),
            name="sums",
            out_shape=pltpu.VMEM(shape, BF16),
            in_specs=[any_spec] * 2,
            out_specs=vmem_spec,
            scratch_shapes=[
                pltpu.VMEM((s["mats"], d, s["tokens"]), BF16),
                pltpu.VMEM((s["chunks"], s["chunk"], d), BF16),
                pltpu.VMEM((3, s["tokens"], tile), BF16),
                pltpu.VMEM((3, tiles, d, tile), BF16),
                pltpu.VMEM((2, tiles, half, tile), BF16),
                pltpu.VMEM((4, tiles, d, tile), BF16),
                pltpu.VMEM((tiles, half, tile), BF16),
                pltpu.VMEM((2, d, tile), BF16),
                pltpu.VMEM((d, tile), F32),
                dma((s["chunks"],)), dma((3,)), dma((2,)), dma((5, tiles)),
                dma((4, tiles)), dma((4, tiles)),
                dma((chips - 1, tiles)), dma((chips - 1, tiles)), dma((chips, tiles)), dma((chips, tiles)),
            ],
            compiler_params=pltpu.CompilerParams(
                collective_id=0, has_side_effects=True, vmem_limit_bytes=50 * 2**20),
        )(a, g)
        return pl.pallas_call(
            store_kernel,
            name="store",
            out_shape=jax.ShapeDtypeStruct(shape, BF16),
            in_specs=[vmem_spec],
            out_specs=any_spec,
            scratch_shapes=[dma((shape[0],))],
            compiler_params=pltpu.CompilerParams(vmem_limit_bytes=2**20),
        )(sums)

    return jax.shard_map(
        step, mesh=mesh, in_specs=(P(("rep", "dp")), P(("rep", "dp"))), out_specs=P("rep"), check_vma=False)
```

time: 358 us -> 200 us (0.56)
  blocking collectives: 293 us -> 0 us
  Pallas kernels: 0 us -> 200 us
  matrix products: 64.2 us -> 0 us
    dot_general x1 -> x0, blocking collectives: 293 us -> none  [step(): jnp.einsum('rsntd,rsntf->rndf', a, g, preferred_element_type=jnp.float32)]
    pallas_call x0 -> x2, Pallas kernels: none -> 200 us  [the longest x1 195 us: step(): pl.pallas_call(functools.partial(sum_kernel, n, s), name='sums', out_shap...]
    dot_general x1 -> x0, matrix products: 64.2 us -> none  [step(): jnp.einsum('rsntd,rsntf->rndf', a, g, preferred_element_type=jnp.float32)]
where the time goes in v1:
time: 200 us
  Pallas kernels  200 us (100%)
    pallas_call x1, Pallas kernels, step(): pl.pallas_call(functools.partial(sum_kernel, n, s), name='sums', out_shap...  195 us
    pallas_call x1, Pallas kernels, step(): pl.pallas_call(store_kernel, name='store', out_shape=jax.ShapeDtypeStruct...  4.89 us

profile of v1, /device:TPU:21, one launch (start us, length us, event | category | flops | bytes accessed | tf_op | source)
XLA Modules:
  0.0 200.1 jit_solution(8609211094196816257)
XLA Ops:
  0.0 195.2 %sums.1.x = bf16[4,640,2560]{2,1,0:T(8,128)(2,1)S(1)} custom-call(bf16[4,4096,640]{2,1,0:T(8,128)(2,1)} %bitcast.2, bf16[4,4096,2560]{2,1,0:T(8,128)(2,1)} %bitcast.1.g_hbm), custom_call_target="tpu_custom_call" | custom-call | tf_op jit(solution)/shard_map/sums/pallas_call | solution.py:317
  195.3 4.9 %store.1 = bf16[4,640,2560]{2,1,0:T(8,128)(2,1)} custom-call(bf16[4,640,2560]{2,1,0:T(8,128)(2,1)S(1)} %sums.1.x), custom_call_target="tpu_custom_call" | custom-call | tf_op jit(solution)/shard_map/store/pallas_call | solution.py:340

commit v2 on v1

--- a/solution.py
+++ b/solution.py
@@ -21,12 +21,14 @@
     tile = 256 if width % 256 == 0 else 128
     return dict(
         mats=mats, tokens=tokens, d=d, ff=ff, chips=chips, half=d // 2, width=width, tile=tile,
-        tiles=width // tile, chunk=tokens // 8, chunks=8,
+        tiles=width // tile, chunk=tokens // 16, chunks=16,
     )
 
 
-def sum_kernel(n, s, a_hbm, g_hbm, out, at, araw, gbuf, part, part_half, land, head, psend, acc,
-               a_sem, g_sem, ps_sem, pr_sem, rs_send, rs_recv, ag_send, ag_recv, ad_send, ad_recv):
+def sum_kernel(n, s, a_hbm, g_hbm, out, at0, at1, at2, at3, araw, gbuf, part, part_half, land, psend, acc,
+               a_sem, g_sem, g0_sem, ps_sem, pr_sem, rs_send, rs_recv, ag_send, ag_recv, ad_send, ad_recv):
+    at = (at0, at1, at2, at3)
+    ring = araw.shape[0]
     mats, chips, half, tile, tiles = s["mats"], s["chips"], s["half"], s["tile"], s["tiles"]
     d, width, chunk, chunks = s["d"], s["width"], s["chunk"], s["chunks"]
     far = chips // 2
@@ -45,16 +47,24 @@
     def shard(r):
         return (c + sgn * r + big) % chips
 
-    def slot_of(r):
-        return (r + big) % mats
-
     def columns(j, i):
         return pl.ds(pl.multiple_of((j // mats) * width + i * tile, tile), tile)
 
-    def a_copy(slot, r):
-        m = (c + sgn * slot + big) % mats
+    order = (0, 1, 3, 2)
+
+    def a_copy(n):
+        m = (c + sgn * order[n // chunks] + big) % mats
         return pltpu.make_async_copy(
-            a_hbm.at[m, pl.ds(pl.multiple_of(r * chunk, chunk), chunk)], araw.at[r], a_sem.at[r])
+            a_hbm.at[m, pl.ds(n % chunks * chunk, chunk)], araw.at[n % ring], a_sem.at[n % ring])
+
+    def late(r):
+        return (3 * chunks + r) % ring
+
+    def late_copy(r):
+        return pltpu.make_async_copy(a_hbm.at[0, pl.ds(0, chunk)], araw.at[late(r)], a_sem.at[late(r)])
+
+    def transpose(n):
+        at[order[n // chunks]][n % chunks] = araw[n % ring].T
 
     def g_copy(q, j, i):
         b = q % depth
@@ -79,12 +89,15 @@
     def g_wait(q):
         g_copy(q, 0, 0).wait()
 
-    def transpose(slot, r):
-        a_copy(slot, r).wait()
-        at[slot, :, pl.ds(pl.multiple_of(r * chunk, chunk), chunk)] = araw[r].T
-
-    def dot(slot, row, rows, q):
-        return jnp.dot(at[slot, pl.ds(row, rows), :], gbuf[q % depth], preferred_element_type=F32)
+    def dot(slot, b, row, rows, t0=0, t1=chunks):
+        lhs = jnp.concatenate([at[slot][t, pl.ds(row, rows), :] for t in range(t0, t1)], axis=1)
+        return jnp.dot(lhs, gbuf[b, pl.ds(t0 * chunk, (t1 - t0) * chunk), :], preferred_element_type=F32)
+
+    def dots(slot, q, t0=0, t1=chunks):
+        return [dot(slot, q % depth, row, half, t0, t1) for row in (other, mine)]
+
+    def held(i):
+        return pl.ds(i % 2 * half, half)
 
     def to_partner(src, dst, u, k, i):
         return pltpu.make_async_remote_copy(
@@ -98,7 +111,7 @@
 
     def rs_head(i):
         return pltpu.make_async_remote_copy(
-            head.at[i], land.at[far - 1, i, pl.ds(mine, half)], rs_send.at[far - 1, i],
+            part_half.at[1, i], land.at[far - 1, i, pl.ds(mine, half)], rs_send.at[far - 1, i],
             rs_recv.at[far - 1, i], device_id=nxt, device_id_type=MESH)
 
     def rs_full(k, i):
@@ -129,107 +142,123 @@
         return pltpu.make_async_remote_copy(
             b, b, ad_send.at[h, i], ad_recv.at[h, i], device_id=partner, device_id_type=MESH)
 
-    for r in range(chunks):
-        a_copy(0, r).start()
-    g_start(0)
-    g_start(1)
+    def g_head(t):
+        rows = pl.ds(t * chunk, chunk)
+        j = shard(far)
+        return pltpu.make_async_copy(g_hbm.at[j % mats, rows, columns(j, 0)], gbuf.at[0, rows], g0_sem.at[t])
+
+    for t in range(chunks):
+        a_copy(t).start()
+        g_head(t).start()
     barrier = pltpu.get_barrier_semaphore()
     for peer in (nxt, prv, partner):
         pl.semaphore_signal(barrier, 1, device_id=peer, device_id_type=MESH)
-    pl.semaphore_wait(barrier, 3)
-
-    def first(r, _):
-        transpose(0, r)
-        a_copy(1, r).start()
-        return 0
-
-    lax.fori_loop(0, chunks, first, 0)
 
     def head_out(i):
         half_p(i % 2, far, i).wait_recv()
-        head[i] = (acc[pl.ds(0, half)] + part_half[1, i].astype(F32)).astype(BF16)
+        part_half[1, i] = (acc[held(i)] + part_half[1, i].astype(F32)).astype(BF16)
         rs_head(i).start()
 
-    def phase_far(i, _):
-        g_start(i + 2)
-        g_wait(i)
-
-        @pl.when(i >= 2)
-        def _():
+    span = chunks // 4
+    for t in range(0, chunks, span):
+        for r in range(t, t + span):
+            a_copy(r).wait()
+            g_head(r).wait()
+            transpose(r)
+        if t == span:
+            g_start(1)
+        if t + span == chunks:
+            for r in range(chunks, chunks + ring):
+                a_copy(r).start()
+            g_start(2)
+        x, y = dots(0, 0, t, t + span)
+        acc[held(1)] = x if t == 0 else acc[held(1)] + x
+        acc[held(0)] = y if t == 0 else acc[held(0)] + y
+
+    extras = ((), (), range(16, 30), range(30, 34), range(34, 48))
+    for i in range(tiles):
+        if i > 0:
+            g_start(i + 2)
+            for n_ in extras[i]:
+                a_copy(n_).wait()
+            g_wait(i)
+            for n_ in extras[i]:
+                transpose(n_)
+            x, acc[held(i)] = dots(0, i)
+        else:
+            x = acc[held(1)]
+        if i >= 2:
             half_p(i % 2, far, i).wait_send()
-
-        psend[i % 2, pl.ds(0, half)] = dot(0, other, half, i).astype(BF16)
+        psend[i % 2, pl.ds(0, half)] = x.astype(BF16)
+        if i == 0:
+            pl.semaphore_wait(barrier, 3)
         half_p(i % 2, far, i).start()
-
-        @pl.when(i >= 1)
-        def _():
+        if i >= 1:
             head_out(i - 1)
-
-        acc[pl.ds(0, half)] = dot(0, mine, half, i)
-
-        @pl.when(i < 4)
-        def _():
-            for u in range(4):
-                r = (4 * i + u) % chunks
-                transpose(1 + 2 * (i // 2), r)
-                a_copy(3 - i // 2, r).start()
-        return 0
-
-    lax.fori_loop(0, tiles, phase_far, 0)
-    head_out(tiles - 1)
-    for u in range(2):
-        half_p(u, far, 0).wait_send()
-
-    def phase(t, _):
-        k = 3 - t // tiles
-        i = t % tiles
+        for n_ in extras[i]:
+            if n_ + ring < 4 * chunks:
+                a_copy(n_ + ring).start()
+
+    def phase(k, i, _):
+        t = (3 - k) * tiles + i
         q = tiles + 2 * t
+
+        def late_chunks(u):
+            if k < 3:
+                return
+            for v in range(u, u + 2):
+                r = 4 * (i - i // 4) + v
+
+                @pl.when(i < 4)
+                def _():
+                    late_copy(r).wait()
+            for v in range(u, u + 2):
+                r = 4 * (i - i // 4) + v
+                at2[r] = araw[late(r)].T
+
         g_start(q + 2)
         g_wait(q)
+        late_chunks(0)
+        x, y = dots(-k % mats, q)
+        if k == 3:
+            @pl.when(i < 2)
+            def _():
+                half_p(t % 2, far, i).wait_send()
 
         @pl.when(t >= 2)
         def _():
             full_p(t % 2, k, i).wait_send()
 
-        psend[t % 2] = dot(slot_of(-k), 0, d, q).astype(BF16)
+        psend[t % 2, pl.ds(other, half)] = x.astype(BF16)
+        psend[t % 2, pl.ds(mine, half)] = y.astype(BF16)
         full_p(t % 2, k, i).start()
-
-        @pl.when(t < 4)
-        def _():
-            for u in range(2):
-                transpose(2, 2 * t + u)
+        if k == 3:
+            @pl.when(i == 0)
+            def _():
+                head_out(tiles - 1)
 
         g_start(q + 3)
         g_wait(q + 1)
-        acc[...] = dot(slot_of(k), 0, d, q + 1)
+        late_chunks(2)
+        acc[pl.ds(other, half)], acc[pl.ds(mine, half)] = dots(k % mats, q + 1)
         full_p(t % 2, k, i).wait_recv()
-
-        @pl.when(k == 3)
-        def _():
-            rs_head(i).wait_recv()
-            land[k, i, pl.ds(mine, half)] = (
-                acc[pl.ds(mine, half)] + part[k - 1, i, pl.ds(mine, half)].astype(F32)
-                + land[k, i, pl.ds(mine, half)].astype(F32)).astype(BF16)
-            land[k, i, pl.ds(other, half)] = (
-                acc[pl.ds(other, half)] + part[k - 1, i, pl.ds(other, half)].astype(F32)).astype(BF16)
-
-        @pl.when(k < 3)
-        def _():
-            rs_full(k + 1, i).wait_recv()
-            land[k, i] = (acc[...] + part[k - 1, i].astype(F32) + land[k, i].astype(F32)).astype(BF16)
-
+        (rs_head(i) if k == 3 else rs_full(k + 1, i)).wait_recv()
+        for row in (other, mine):
+            x = acc[pl.ds(row, half)] + part[k - 1, i, pl.ds(row, half)].astype(F32)
+            if k < 3 or row is mine:
+                x = x + land[k, i, pl.ds(row, half)].astype(F32)
+            land[k, i, pl.ds(row, half)] = x.astype(BF16)
         rs_full(k, i).start()
         return 0
 
-    lax.fori_loop(0, 3 * tiles, phase, 0)
-    for u in range(2):
-        full_p(u, 1, 0).wait_send()
+    for k in (3, 2, 1):
+        lax.fori_loop(0, tiles, functools.partial(phase, k), 0)
 
     def own_out(i):
         half_p(i % 2, 0, i).wait_recv()
         j = shard(0)
         out[j % mats, pl.ds(mine, half), columns(j, i)] = (
-            acc[pl.ds(0, half)] + part_half[0, i].astype(F32)).astype(BF16)
+            acc[held(i)] + land[0, i, pl.ds(mine, half)].astype(F32) + part_half[0, i].astype(F32)).astype(BF16)
         ag(1, i).start()
         across(0, i).start()
 
@@ -237,21 +266,24 @@
         q = 7 * tiles + i
         g_start(q + 2)
         g_wait(q)
+        x, acc[held(i)] = dots(0, q)
+
+        @pl.when(i < 2)
+        def _():
+            full_p(i % 2, 1, 0).wait_send()
 
         @pl.when(i >= 2)
         def _():
             half_p(i % 2, 0, i).wait_send()
 
         rs_full(1, i).wait_recv()
-        psend[i % 2, pl.ds(0, half)] = (
-            dot(0, other, half, q) + land[0, i, pl.ds(other, half)].astype(F32)).astype(BF16)
+        psend[i % 2, pl.ds(0, half)] = (x + land[0, i, pl.ds(other, half)].astype(F32)).astype(BF16)
         half_p(i % 2, 0, i).start()
 
         @pl.when(i >= 1)
         def _():
             own_out(i - 1)
 
-        acc[pl.ds(0, half)] = dot(0, mine, half, q) + land[0, i, pl.ds(mine, half)].astype(F32)
         return 0
 
     lax.fori_loop(0, tiles, phase_own, 0)
@@ -296,7 +328,9 @@
 
 
 def store_kernel(x, o, sem):
-    parts = [pltpu.make_async_copy(x.at[m], o.at[m], sem.at[m]) for m in range(x.shape[0])]
+    rows = x.shape[1] // 4
+    blocks = [(m, pl.ds(r * rows, rows)) for m in range(x.shape[0]) for r in range(4)]
+    parts = [pltpu.make_async_copy(x.at[b], o.at[b], sem.at[i]) for i, b in enumerate(blocks)]
     for p in parts:
         p.start()
     for p in parts:
@@ -321,21 +355,20 @@
             in_specs=[any_spec] * 2,
             out_specs=vmem_spec,
             scratch_shapes=[
-                pltpu.VMEM((s["mats"], d, s["tokens"]), BF16),
-                pltpu.VMEM((s["chunks"], s["chunk"], d), BF16),
+                *[pltpu.VMEM((s["chunks"], d, s["chunk"]), BF16) for _ in range(s["mats"])],
+                pltpu.VMEM((18, s["chunk"], d), BF16),
                 pltpu.VMEM((3, s["tokens"], tile), BF16),
                 pltpu.VMEM((3, tiles, d, tile), BF16),
                 pltpu.VMEM((2, tiles, half, tile), BF16),
                 pltpu.VMEM((4, tiles, d, tile), BF16),
-                pltpu.VMEM((tiles, half, tile), BF16),
                 pltpu.VMEM((2, d, tile), BF16),
                 pltpu.VMEM((d, tile), F32),
-                dma((s["chunks"],)), dma((3,)), dma((2,)), dma((5, tiles)),
+                dma((18,)), dma((3,)), dma((s["chunks"],)), dma((2,)), dma((5, tiles)),
                 dma((4, tiles)), dma((4, tiles)),
                 dma((chips - 1, tiles)), dma((chips - 1, tiles)), dma((chips, tiles)), dma((chips, tiles)),
             ],
             compiler_params=pltpu.CompilerParams(
-                collective_id=0, has_side_effects=True, vmem_limit_bytes=50 * 2**20),
+                collective_id=0, has_side_effects=True, vmem_limit_bytes=53_800_000),
         )(a, g)
         return pl.pallas_call(
             store_kernel,
@@ -343,7 +376,7 @@
             out_shape=jax.ShapeDtypeStruct(shape, BF16),
             in_specs=[vmem_spec],
             out_specs=any_spec,
-            scratch_shapes=[dma((shape[0],))],
+            scratch_shapes=[dma((4 * shape[0],))],
             compiler_params=pltpu.CompilerParams(vmem_limit_bytes=2**20),
         )(sums)
 

time: 200 us -> 153 us (0.77)
  Pallas kernels: 200 us -> 153 us
    pallas_call x1, Pallas kernels: 195 us -> 148 us  [step(): pl.pallas_call(functools.partial(sum_kernel, n, s), name='sums', out_shap...]
where the time goes in v2:
time: 153 us
  Pallas kernels  153 us (100%)
    pallas_call x1, Pallas kernels, step(): pl.pallas_call(functools.partial(sum_kernel, n, s), name='sums', out_shap...  148 us
    pallas_call x1, Pallas kernels, step(): pl.pallas_call(store_kernel, name='store', out_shape=jax.ShapeDtypeStruct...  4.87 us

profile of v2, /device:TPU:21, one launch (start us, length us, event | category | flops | bytes accessed | tf_op | source)
XLA Modules:
  0.0 152.8 jit_solution(13926362458803016894)
XLA Ops:
  0.0 147.8 %sums.1.x = bf16[4,640,2560]{2,1,0:T(8,128)(2,1)S(1)} custom-call(bf16[4,4096,640]{2,1,0:T(8,128)(2,1)} %bitcast.2, bf16[4,4096,2560]{2,1,0:T(8,128)(2,1)} %bitcast.1.g_hbm), custom_call_target="tpu_custom_call" | custom-call | tf_op jit(solution)/shard_map/sums/pallas_call | solution.py:351
  147.8 4.9 %store.1 = bf16[4,640,2560]{2,1,0:T(8,128)(2,1)} custom-call(bf16[4,640,2560]{2,1,0:T(8,128)(2,1)S(1)} %sums.1.x), custom_call_target="tpu_custom_call" | custom-call | tf_op jit(solution)/shard_map/store/pallas_call | solution.py:373
